TPU v7x, 32 devices: a whole 2x2x4 slice. The times are simulated.
32 devices in a mesh: samp: 8 (over z, x), win: 1, snp: 4 (over y, core).
Axes of the slice: x: 2, y: 2, z: 4, core: 2. Of those that a mesh axis runs over, the one named last changes fastest.
Arguments:
- dosages: bfloat16 [4096, 4096], P('samp', ('win', 'snp')), may hold values from 0 to 2
Outputs:
- r_squared: float32 [1, 4096, 4096], P('win', 'samp', 'snp')
- band_r_squared: float32 [1, 1024, 4096], P('win', 'samp', 'snp')
All inputs are finite; a program needn't handle non-finite values.
Results may differ from a plain program's by a relative error of at most 0.0003.
Values may be sent and summed in bfloat16 or wider, within the bound.
A program may use at most 128 MiB of HBM per device.

v0:
```python
import jax
import jax.numpy as jnp
from jax import lax
from jax.sharding import PartitionSpec as P

OV = 1024
var_floor = 0.05


def passed_along(shard, axis, by):
    devices = lax.axis_size(axis)
    return lax.ppermute(shard, axis, [(i, (i + by) % devices) for i in range(devices)])


def squared_corr(gram, col_sum, col_sq, row_sum, row_sq, count):
    col_mean = col_sum / count
    row_mean = row_sum / count
    col_var = jnp.maximum(col_sq / count - col_mean * col_mean, var_floor)
    row_var = jnp.maximum(row_sq / count - row_mean * row_mean, var_floor)
    covar = gram / count - col_mean[:, None] * row_mean[None, :]
    return covar * covar / (col_var[:, None] * row_var[None, :])


def column_stats(block):
    return (
        jnp.sum(block, axis=0, dtype=jnp.float32),
        jnp.sum(jnp.square(block.astype(jnp.float32)), axis=0),
    )


def pair_sums(columns, own_rows):
    return lax.dot_general(
        columns, own_rows, (((0,), (0,)), ((), ())), preferred_element_type=jnp.float32
    )


def shards(dosages):
    samples_here = dosages.shape[0]
    block_width = dosages.shape[1]
    shard_count = lax.axis_size("samp")
    count = jnp.float32(samples_here * shard_count)
    whole = lax.all_gather(dosages, "snp", axis=1, tiled=True)
    window_width = whole.shape[1]
    band = passed_along(whole[:, :OV], "win", -1)
    own_sum, own_sq = column_stats(dosages)
    total_sum, total_sq = lax.psum((own_sum, own_sq), "samp")
    win_sum, win_sq = (
        lax.all_gather(total_sum, "snp", axis=0, tiled=True),
        lax.all_gather(total_sq, "snp", axis=0, tiled=True),
    )
    next_sum, next_sq = passed_along((win_sum[:OV], win_sq[:OV]), "win", -1)
    win_cols = window_width // shard_count
    band_cols = OV // shard_count
    merged = jnp.concatenate(
        (
            whole.reshape(samples_here, shard_count, win_cols),
            band.reshape(samples_here, shard_count, band_cols),
        ),
        axis=2,
    ).reshape(samples_here, shard_count * (win_cols + band_cols))
    summed = lax.psum_scatter(pair_sums(merged, dosages), "samp", scatter_dimension=0, tiled=True)
    win_gram = summed[:win_cols]
    band_gram = summed[win_cols:]
    col_index = lax.axis_index("samp")
    row_index = lax.axis_index("snp")
    row_sum = lax.dynamic_slice_in_dim(win_sum, row_index * block_width, block_width, 0)
    row_sq = lax.dynamic_slice_in_dim(win_sq, row_index * block_width, block_width, 0)
    col_sum = lax.dynamic_slice_in_dim(win_sum, col_index * win_cols, win_cols, 0)
    col_sq = lax.dynamic_slice_in_dim(win_sq, col_index * win_cols, win_cols, 0)
    band_sum = lax.dynamic_slice_in_dim(next_sum, col_index * band_cols, band_cols, 0)
    band_sq = lax.dynamic_slice_in_dim(next_sq, col_index * band_cols, band_cols, 0)
    whole_out = squared_corr(win_gram, col_sum, col_sq, row_sum, row_sq, count)
    band_out = squared_corr(band_gram, band_sum, band_sq, row_sum, row_sq, count)
    return (whole_out[None], band_out[None])


def solution(mesh):
    return jax.shard_map(
        shards,
        mesh=mesh,
        in_specs=(P("samp", ("win", "snp")),),
        out_specs=(P("win", "samp", "snp"), P("win", "samp", "snp")),
        check_vma=False,
    )
```

profile of v0, /device:TPU:0, one launch (start us, length us, event | category | flops | bytes accessed | tf_op | source)
XLA Modules:
  0.0 419.4 jit_solution(9305339508099588703)
XLA Ops:
  7.2 0.0 all-gather.2.cloned.1.call-start
  7.2 0.7 all-gather.2.cloned.1.call-update
  7.9 0.0 reduce-scatter.2.cloned.1.call-start
  7.9 38.8 %all-gather.2.cloned.1.call-done = bf16[512,4096]{1,0:T(8,128)(2,1)} async-done(((bf16[512,1024]{1,0:T(8,128)(2,1)}), bf16[512,4096]{1,0:T(8,128)(2,1)}) %all-gather.2.cloned.1.call-update) | async-done | bytes 4194320 | tf_op jit(solution)/shard_map/all_gather | solution.py:42
  46.8 1.3 slice.20
  48.0 0.1 collective-permute-start
  48.1 4.4 %copy.3 = bf16[64,8,8,512]{3,2,1,0:T(8,128)(2,1)S(1)} copy(bf16[64,8,8,512]{3,1,2,0:T(8,128)(2,1)} %bitcast.14) | data formatting | bytes 8388608
  52.5 0.0 collective-permute-done
  52.6 0.3 copy.4
  52.8 0.5 pad_maximum_fusion
  53.3 0.0 copy-start
  53.3 1.2 copy.5
  54.5 0.0 copy-done
  54.5 9.9 %fusion.10 = f32[5120,1024]{1,0:T(8,128)} fusion(bf16[512,5120]{1,0:T(8,128)(2,1)S(1)} %bitcast.15, bf16[512,1024]{1,0:T(8,128)(2,1)S(1)} %copy-done), kind=kOutput, calls=%fused_computation.21 | convolution fusion | flops 5368709120 | bytes 27262976 | tf_op jit(solution)/shard_map/dot_general | solution.py:32
  64.4 0.0 reduce-scatter.2.cloned.1.call-update
  64.4 0.3 convert_reduce_fusion
  64.8 22.7 %all-reduce = (f32[1024]{0:T(1024)S(1)}, f32[1024]{0:T(1024)S(1)}) all-reduce(f32[1024]{0:T(1024)S(1)} %get-tuple-element.3, f32[1024]{0:T(1024)S(1)} %get-tuple-element.2), channel_id=1, replica_groups=mesh['samp'=8,'win'=1,'snp'=4] {'samp'}, use_global_device_ids=true, to_apply=%region_4.0 | all-reduce | flops 2048 | bytes 16384 | tf_op jit(solution)/shard_map/psum | solution.py:46
  87.5 5.2 %all_gather.10 = f32[4096]{0:T(1024)S(1)} all-gather(f32[1024]{0:T(1024)S(1)} %get-tuple-element.5), channel_id=1, replica_groups=mesh['samp'=8,'win'=1,'snp'=4] {'snp'}, dimensions={0}, use_global_device_ids=true | all-gather | bytes 20480 | tf_op jit(solution)/shard_map/all_gather | solution.py:48
  92.7 5.2 %all_gather.11 = f32[4096]{0:T(1024)S(1)} all-gather(f32[1024]{0:T(1024)S(1)} %get-tuple-element.4), channel_id=1, replica_groups=mesh['samp'=8,'win'=1,'snp'=4] {'snp'}, dimensions={0}, use_global_device_ids=true | all-gather | bytes 20480 | tf_op jit(solution)/shard_map/all_gather | solution.py:49
  97.9 0.0 collective-permute-start.1
  97.9 0.0 collective-permute-start.2
  97.9 0.1 dynamic-slice_multiply_fusion.1
  98.0 0.0 collective-permute-done.1
  98.0 0.0 collective-permute-done.2
  98.0 0.1 dynamic-slice_multiply_fusion.2
  98.1 308.9 %reduce-scatter.2.cloned.1.call-done = f32[640,1024]{1,0:T(8,128)} async-done(((f32[5120,1024]{1,0:T(8,128)}), f32[640,1024]{1,0:T(8,128)}) %reduce-scatter.2.cloned.1.call-update) | async-done | bytes 2621456 | tf_op jit(solution)/shard_map/reduce_scatter | solution.py:61
  407.0 3.5 fusion.4
  410.5 2.0 fusion.8
  (1 shorter events, 0.0 us)
Async XLA Ops:
  7.2 39.6 %all-gather.2.cloned.1.call-start = ((), (), s32[]{:S(2)}) async-start(), calls=%async_computation.1 | async-start | bytes 5242880 | tf_op jit(solution)/shard_map/all_gather | solution.py:42
  7.9 399.1 %reduce-scatter.2.cloned.1.call-start = ((), (), s32[]{:S(2)}) async-start(), calls=%async_computation.2 | async-start | bytes 23592960 | tf_op jit(solution)/shard_map/reduce_scatter | solution.py:61
  48.0 4.5 %collective-permute-start = (bf16[512,1024]{1,0:T(8,128)(2,1)S(1)}, bf16[512,1024]{1,0:T(8,128)(2,1)S(1)}, u32[]{:S(2)}, u32[]{:S(2)}) collective-permute-start(bf16[512,1024]{1,0:T(8,128)(2,1)S(1)} %slice.20), channel_id=1, source_target_pairs={{0,0},{1,1},{2,2},{3,3},{4,4},{5,5},{6,6},{7,7},{8,8},{9,9},{10,10... | collective-permute-start | bytes 3145736 | tf_op jit(solution)/shard_map/ppermute | solution.py:12
  53.3 1.2 copy-start
  97.9 0.1 collective-permute-start.1
  97.9 0.1 collective-permute-start.2
Sparse Core Ops, SparseCore 0:
  9.5 37.1 all-gather.1
  64.6 342.4 reduce-scatter.1
where the time goes:
time: 420 us; the launch traced here: 419 us
  waiting for transfers between devices  348 us (83%)
  blocking collectives  33.1 us (8%)
  between operations  14.1 us (3%)
  matrix products  9.9 us (2%)
  local copies, waits for them, and re-layouts  7.19 us (2%)
  other arithmetic  6.47 us (2%)
    reduce_scatter x1, waiting for transfers between devices, shards(): lax.psum_scatter(pair_sums(merged, dosages), 'samp', scatter_dimension=0,...  309 us
    all_gather x1, waiting for transfers between devices, shards(): whole = lax.all_gather(dosages, 'snp', axis=1, tiled=True)  38.8 us
    psum x1, blocking collectives, shards(): total_sum, total_sq = lax.psum((own_sum, own_sq), 'samp')  22.7 us
    dot_general x1, matrix products, pair_sums(): lax.dot_general(columns, own_rows, (((0,), (0,)), ((), ())), preferred_el...  9.9 us
  transfers between devices with their start and end apart: 5, of which 2 were waited for; matrix products, arithmetic and copies ran while one was open for 1% of the time, Pallas kernels for 0%

commit v1 on v0

--- a/solution.py
+++ b/solution.py
@@ -39,7 +39,12 @@
     block_width = dosages.shape[1]
     shard_count = lax.axis_size("samp")
     count = jnp.float32(samples_here * shard_count)
-    whole = lax.all_gather(dosages, "snp", axis=1, tiled=True)
+    ring = [dosages]
+    for hop in range(3):
+        ring.append(lax.ppermute(ring[-1], "snp", [(dev, (dev + 1) % 4) for dev in range(4)]))
+    whole = jnp.roll(
+        jnp.concatenate(ring[::-1], axis=1), (lax.axis_index("snp") + 1) * ring[0].shape[1], axis=1
+    )
     window_width = whole.shape[1]
     band = passed_along(whole[:, :OV], "win", -1)
     own_sum, own_sq = column_stats(dosages)

time: 420 us -> 428 us (1.019)
  waiting for transfers between devices: 348 us -> 354 us
    ppermute x0 -> x3, waiting for transfers between devices: none -> 43.1 us  [shards(): lax.ppermute(ring[-1], 'snp', [(dev, (dev + 1) % 4) for dev in range(4)])]
    all_gather x1 -> x0, waiting for transfers between devices: 38.8 us -> none  [shards(): whole = lax.all_gather(dosages, 'snp', axis=1, tiled=True)]
  transfers between devices with their start and end apart: 5 -> 7, of which waited for: 2 -> 4; matrix products, arithmetic and copies ran while one was open for 1% -> 1% of each run, Pallas kernels for 0% -> 0%
where the time goes in v1:
time: 428 us
  waiting for transfers between devices  354 us (83%)
  blocking collectives  33.9 us (8%)
  between operations  14.2 us (3%)
  matrix products  9.92 us (2%)
  local copies, waits for them, and re-layouts  8.27 us (2%)
  other arithmetic  6.47 us (2%)
    reduce_scatter x1, waiting for transfers between devices, shards(): lax.psum_scatter(pair_sums(merged, dosages), 'samp', scatter_dimension=0,...  311 us
    ppermute x3, waiting for transfers between devices, shards(): lax.ppermute(ring[-1], 'snp', [(dev, (dev + 1) % 4) for dev in range(4)])  43.1 us
    psum x1, blocking collectives, shards(): total_sum, total_sq = lax.psum((own_sum, own_sq), 'samp')  23.5 us
    dot_general x1, matrix products, pair_sums(): lax.dot_general(columns, own_rows, (((0,), (0,)), ((), ())), preferred_el...  9.92 us
  transfers between devices with their start and end apart: 7, of which 4 were waited for; matrix products, arithmetic and copies ran while one was open for 1% of the time, Pallas kernels for 0%

profile of v1, /device:TPU:0, one launch (start us, length us, event | category | flops | bytes accessed | tf_op | source)
XLA Modules:
  0.0 427.7 jit_solution(14432920104413196290)
XLA Ops:
  7.2 0.0 reduce-scatter.2.cloned.1.call-start
  7.2 0.5 collective-permute-start
  7.8 14.6 %collective-permute-done = bf16[512,1024]{1,0:T(8,128)(2,1)S(1)} collective-permute-done((bf16[512,1024]{1,0:T(8,128)(2,1)}, bf16[512,1024]{1,0:T(8,128)(2,1)S(1)}, u32[]{:S(2)}, u32[]{:S(2)}) %collective-permute-start) | collective-permute-done | bytes 1048608 | tf_op jit(solution)/shard_map/ppermute | solution.py:44
  22.4 0.0 collective-permute-start.1
  22.4 14.2 %collective-permute-done.1 = bf16[512,1024]{1,0:T(8,128)(2,1)S(1)} collective-permute-done((bf16[512,1024]{1,0:T(8,128)(2,1)S(1)}, bf16[512,1024]{1,0:T(8,128)(2,1)S(1)}, u32[]{:S(2)}, u32[]{:S(2)}) %collective-permute-start.1) | collective-permute-done | bytes 1048608 | tf_op jit(solution)/shard_map/ppermute | solution.py:44
  36.6 14.3 %collective-permute-done.2 = bf16[512,1024]{1,0:T(8,128)(2,1)} collective-permute-done((bf16[512,1024]{1,0:T(8,128)(2,1)S(1)}, bf16[512,1024]{1,0:T(8,128)(2,1)}, u32[]{:S(2)}, u32[]{:S(2)}) %collective-permute-start.2) | collective-permute-done | bytes 1048608 | tf_op jit(solution)/shard_map/ppermute | solution.py:44
  51.0 1.3 constant_dynamic-update-slice_fusion.7
  52.3 0.1 constant_dynamic-update-slice_fusion.6
  52.3 0.1 constant_dynamic-update-slice_fusion.5
  52.4 1.3 constant_dynamic-update-slice_fusion.4
  53.7 1.3 constant_dynamic-update-slice_fusion.3
  55.0 0.1 constant_dynamic-update-slice_fusion.2
  55.1 0.1 constant_dynamic-update-slice_fusion.1
  55.2 0.1 constant_dynamic-update-slice_fusion
  55.3 0.1 constant_dynamic-slice_fusion
  55.3 0.1 collective-permute-start.3
  55.4 0.3 constant_dynamic-slice_fusion.1
  55.7 2.2 copy.3
  58.0 0.3 copy.4
  58.2 0.5 pad_maximum_fusion
  58.7 1.2 copy.5
  59.9 9.9 %fusion.10 = f32[5120,1024]{1,0:T(8,128)} fusion(bf16[512,5120]{1,0:T(8,128)(2,1)S(1)} %bitcast.15, bf16[512,1024]{1,0:T(8,128)(2,1)S(1)} %copy-done), kind=kOutput, calls=%fused_computation.31 | convolution fusion | flops 5368709120 | bytes 27262976 | tf_op jit(solution)/shard_map/dot_general | solution.py:32
  69.8 0.0 reduce-scatter.2.cloned.1.call-update
  69.8 0.3 convert_reduce_fusion
  70.1 23.5 %all-reduce = (f32[1024]{0:T(1024)S(1)}, f32[1024]{0:T(1024)S(1)}) all-reduce(f32[1024]{0:T(1024)S(1)} %get-tuple-element.3, f32[1024]{0:T(1024)S(1)} %get-tuple-element.2), channel_id=1, replica_groups=mesh['samp'=8,'win'=1,'snp'=4] {'samp'}, use_global_device_ids=true, to_apply=%region_4.5 | all-reduce | flops 2048 | bytes 16384 | tf_op jit(solution)/shard_map/psum | solution.py:51
  93.7 5.2 %all_gather.6 = f32[4096]{0:T(1024)S(1)} all-gather(f32[1024]{0:T(1024)S(1)} %get-tuple-element.5), channel_id=1, replica_groups=mesh['samp'=8,'win'=1,'snp'=4] {'snp'}, dimensions={0}, use_global_device_ids=true | all-gather | bytes 20480 | tf_op jit(solution)/shard_map/all_gather | solution.py:53
  98.9 5.2 %all_gather.7 = f32[4096]{0:T(1024)S(1)} all-gather(f32[1024]{0:T(1024)S(1)} %get-tuple-element.4), channel_id=1, replica_groups=mesh['samp'=8,'win'=1,'snp'=4] {'snp'}, dimensions={0}, use_global_device_ids=true | all-gather | bytes 20480 | tf_op jit(solution)/shard_map/all_gather | solution.py:54
  104.1 0.1 dynamic-slice_multiply_fusion.1
  104.2 0.1 dynamic-slice_multiply_fusion.2
  104.3 311.0 %reduce-scatter.2.cloned.1.call-done = f32[640,1024]{1,0:T(8,128)} async-done(((f32[5120,1024]{1,0:T(8,128)}), f32[640,1024]{1,0:T(8,128)}) %reduce-scatter.2.cloned.1.call-update) | async-done | bytes 2621456 | tf_op jit(solution)/shard_map/reduce_scatter | solution.py:66
  415.3 3.5 fusion.4
  418.8 2.0 fusion.8
  (9 shorter events, 0.0 us)
Async XLA Ops:
  7.2 48.0 %copy-start = (bf16[512,1024]{1,0:T(8,128)(2,1)S(1)}, bf16[512,1024]{1,0:T(8,128)(2,1)}, u32[]{:S(2)}) copy-start(bf16[512,1024]{1,0:T(8,128)(2,1)} %param.1) | copy-start | bytes 3145732
  7.2 408.1 %reduce-scatter.2.cloned.1.call-start = ((), (), s32[]{:S(2)}) async-start(), calls=%async_computation.1 | async-start | bytes 23592960 | tf_op jit(solution)/shard_map/reduce_scatter | solution.py:66
  7.2 15.2 %collective-permute-start = (bf16[512,1024]{1,0:T(8,128)(2,1)}, bf16[512,1024]{1,0:T(8,128)(2,1)S(1)}, u32[]{:S(2)}, u32[]{:S(2)}) collective-permute-start(bf16[512,1024]{1,0:T(8,128)(2,1)} %param.1), channel_id=1, source_target_pairs={{0,1},{1,2},{2,3},{3,0},{4,5},{5,6},{6,7},{7,4},{8,9},{9,10},{10,1... | collective-permute-start | bytes 3145736 | tf_op jit(solution)/shard_map/ppermute | solution.py:44
  22.4 14.2 %collective-permute-start.1 = (bf16[512,1024]{1,0:T(8,128)(2,1)S(1)}, bf16[512,1024]{1,0:T(8,128)(2,1)S(1)}, u32[]{:S(2)}, u32[]{:S(2)}) collective-permute-start(bf16[512,1024]{1,0:T(8,128)(2,1)S(1)} %collective-permute-done), channel_id=1, source_target_pairs={{0,1},{1,2},{2,3},{3,0},{4,5},{5,6},{6,7},{7,4},{8,9},{9,10},{10,1... | collective-permute-start | bytes 3145736 | tf_op jit(solution)/shard_map/ppermute | solution.py:44
  36.6 14.3 %collective-permute-start.2 = (bf16[512,1024]{1,0:T(8,128)(2,1)S(1)}, bf16[512,1024]{1,0:T(8,128)(2,1)}, u32[]{:S(2)}, u32[]{:S(2)}) collective-permute-start(bf16[512,1024]{1,0:T(8,128)(2,1)S(1)} %collective-permute-done.1), channel_id=1, source_target_pairs={{0,1},{1,2},{2,3},{3,0},{4,5},{5,6},{6,7},{7,4},{8,9},{9,10},{10,1... | collective-permute-start | bytes 3145736 | tf_op jit(solution)/shard_map/ppermute | solution.py:44
  55.3 2.6 collective-permute-start.3
  104.1 0.1 collective-permute-start.4
  104.1 0.1 collective-permute-start.5
Sparse Core Ops, SparseCore 0:
  69.9 345.3 reduce-scatter.1
